TPU v7x, 256 devices: a whole 4x4x8 slice. The times are simulated.
256 devices in a mesh: tok: 8 (over z), tile: 16 (over y, x_lo, core), pair: 2 (over x_hi).
Axes of the slice: x: 4 (x_hi: 2, x_lo: 2; x = x_hi * 2 + x_lo), y: 4, z: 8, core: 2. Of those that a mesh axis runs over, the one named last changes fastest.
Arguments:
- inputs: bfloat16 [8192, 4096], P(('tok', 'pair'), 'tile'), may hold values from -6 to 6
- output_grads: bfloat16 [8192, 4096], P(('tok', 'pair'), 'tile'), may hold values from -0.0625 to 0.0625
- statistics: float32 [16, 2, 1024, 1024], P('tile', 'pair', 'tok'), may hold values from -30 to 43008, as said below
Outputs:
- update: bfloat16 [16, 1024, 1024], P('tile', ('tok', 'pair'))
- new_statistics: float32 [16, 2, 1024, 1024], P('tile', 'pair', 'tok')
Inputs may be any that keep to these rules, and one draw needn't show every extreme that they name: `statistics`: for every block and factor the 1024 x 1024 matrix is symmetric and positive definite.
All inputs are finite; a program needn't handle non-finite values. Where the computation divides by a largest or mean magnitude, that divisor is 1e-20 or more.
Results may differ from a plain program's by a relative error of at most 0.00325.
The roundings to bfloat16 on the way count: a program that leaves them out, or rounds other values in their place, can miss the bound.
Values may be sent and summed in bfloat16 or wider, within the bound.
No kernel may reach another device: no remote copies, remote signals or barrier semaphores. Data moves between devices by JAX's collectives and lax.ppermute only.
A program may use at most 64 MiB of HBM per device.

v0:
```python
import jax
import jax.numpy as jnp
import numpy as np
from jax import lax
from jax.sharding import PartitionSpec as P

ITERS = 2


def in_one_piece(arrays, axis, split_dim, concat_dim, along):
    ends, at = ([], 0)
    for a in arrays[:-1]:
        at += a.shape[along]
        ends.append(at)
    both = jnp.concatenate(arrays, axis=along)
    return tuple(
        jnp.split(
            lax.all_to_all(both, axis, split_axis=split_dim, concat_axis=concat_dim, tiled=True),
            ends,
            axis=along,
        )
    )


def swapped(shard, axis, stride):
    return lax.ppermute(shard, axis, [(i, i ^ 1 << stride) for i in range(lax.axis_size(axis))])


def copy_for_each(shard, axis):
    copies = jnp.broadcast_to(shard, (lax.axis_size(axis), *shard.shape))
    return lax.all_to_all(copies, axis, split_axis=0, concat_axis=0, tiled=True)


def of_everyone(shard, axis):
    everything = copy_for_each(shard, axis)
    return jnp.sum(everything, axis=0)


def product_bf(left_part, right_part):
    return jnp.einsum(
        "kab,kbc->kac", left_part, right_part, preferred_element_type=jnp.float32
    ).astype(jnp.bfloat16)


def per_device(inputs, output_grads, statistics):
    blocks = statistics.shape[0]
    state_rows = statistics.shape[2]
    matrix_order = statistics.shape[3]
    tile_count = lax.axis_size("tile")
    model_width = inputs.shape[1] * tile_count
    per_side = model_width // matrix_order
    tok_index = lax.axis_index("tok")
    pair_index = lax.axis_index("pair")
    shard_index = tok_index * lax.axis_size("pair") + pair_index
    devices_block = lax.axis_size("tok") * lax.axis_size("pair")
    out_rows = matrix_order // devices_block
    token_acts, token_cots = (
        lax.all_to_all(inputs, "tile", split_axis=0, concat_axis=1, tiled=True),
        lax.all_to_all(output_grads, "tile", split_axis=0, concat_axis=1, tiled=True),
    )
    slice_tokens = token_acts.shape[0]
    all_blocks = np.arange(tile_count * blocks)
    row_blocks = all_blocks // per_side
    col_blocks = all_blocks % per_side
    acts_blocks = token_acts.reshape(slice_tokens, per_side, matrix_order)[:, row_blocks]
    cots_blocks = token_cots.reshape(slice_tokens, per_side, matrix_order)[:, col_blocks]
    acts_send = acts_blocks.reshape(slice_tokens, tile_count, blocks, matrix_order)
    cots_send = cots_blocks.reshape(slice_tokens, tile_count, blocks, matrix_order)
    acts_mine, cots_mine = in_one_piece((acts_send, cots_send), "tile", 1, 0, 2)
    left_acts = jnp.transpose(acts_mine[:, 0], (1, 0, 2))
    right_cots = jnp.transpose(cots_mine[:, 0], (1, 0, 2))
    partial_grad = jnp.einsum(
        "ktr,ktc->rkc", left_acts, right_cots, preferred_element_type=jnp.float32
    )
    gradient = lax.psum(partial_grad, ("tok", "pair")).astype(jnp.bfloat16)
    grad_sq = jnp.einsum("rkc,rkc->k", gradient, gradient, preferred_element_type=jnp.float32)
    by_rows = jnp.transpose(gradient, (1, 0, 2))
    by_cols = jnp.transpose(gradient, (1, 2, 0))
    factor_data = jnp.where(pair_index == 0, by_rows, by_cols)
    identity = jnp.eye(matrix_order, dtype=jnp.float32)
    row_start = tok_index * state_rows
    previous = lax.all_gather(statistics[:, 0], "tok", axis=1, tiled=True)
    product = jnp.einsum(
        "kac,kbc->kab", factor_data, factor_data, preferred_element_type=jnp.float32
    )
    updated = 0.9 * previous + 0.1 * product
    new_rows = lax.dynamic_slice_in_dim(updated, row_start, state_rows, 1)
    bound_max = jnp.max(jnp.sum(jnp.abs(updated), axis=2), axis=1)[:, None, None]
    iterate = ((updated + 0.1 * bound_max * identity) / (1.1 * bound_max)).astype(jnp.bfloat16)
    iterate = lax.optimization_barrier(iterate)
    root_whole = iterate
    for iteration in range(ITERS):
        factor = ((5.0 * identity - iterate.astype(jnp.float32)) / 4.0).astype(jnp.bfloat16)
        if iteration == 0:
            root_whole = factor
        else:
            root_whole = product_bf(root_whole, factor)
        if iteration + 1 < ITERS:
            square = product_bf(factor, factor)
            fourth = product_bf(square, square)
            iterate = lax.optimization_barrier(product_bf(fourth, iterate))
    partner = swapped(root_whole, "pair", 0)
    left_whole = jnp.where(pair_index == 0, root_whole, partner)
    right_whole = jnp.where(pair_index == 0, partner, root_whole)
    left_part = lax.dynamic_slice_in_dim(left_whole, shard_index * out_rows, out_rows, 1)
    left_mixed = jnp.einsum(
        "kqr,rkc->kqc", left_part, gradient, preferred_element_type=jnp.float32
    ).astype(jnp.bfloat16)
    raw_update = jnp.einsum(
        "kqc,kcd->kqd", left_mixed, right_whole, preferred_element_type=jnp.float32
    )
    local_sq = jnp.sum(raw_update * raw_update, axis=(1, 2))
    update_total = of_everyone(local_sq, ("tok", "pair"))
    graft_ratio = jnp.sqrt(grad_sq / (update_total + 1e-06))
    update = (raw_update * graft_ratio[:, None, None]).astype(jnp.bfloat16)
    return (update, new_rows[:, None])


def solution(mesh):
    placed = (
        P(("tok", "pair"), "tile"),
        P(("tok", "pair"), "tile"),
        P("tile", "pair", "tok", None),
    )
    return jax.shard_map(
        per_device,
        mesh=mesh,
        in_specs=placed,
        out_specs=(P("tile", ("tok", "pair"), None), P("tile", "pair", "tok", None)),
        check_vma=False,
    )
```

profile of v0, /device:TPU:18, one launch (start us, length us, event | category | flops | bytes accessed | tf_op | source)
XLA Modules:
  0.0 368.6 jit_solution(7641497615641156873)
XLA Ops:
  7.2 0.0 copy-start.1
  7.2 0.0 copy-start.2
  7.2 0.0 all-gather.3.cloned.1.call-start
  7.2 2.0 copy.39
  9.3 0.0 all-gather.3.cloned.1.call-update
  9.3 10.3 %all_to_all.56 = bf16[16,32,256]{2,1,0:T(8,128)(2,1)S(1)} all-to-all(bf16[16,32,256]{2,1,0:T(8,128)(2,1)} %bitcast.102), channel_id=1, replica_groups=mesh['tok'=8,'tile'=16,'pair'=2] {'tile'}, dimensions={0} | all-to-all | bytes 524288 | tf_op jit(solution)/shard_map/all_to_all | solution.py:59
  19.6 7.0 %all-to-all-start = ((bf16[16,32,256]{2,1,0:T(8,128)(2,1)}), bf16[16,32,256]{2,1,0:T(8,128)(2,1)S(1)}, u32[]{:S(2)}, u32[]{:S(2)}) async-start(bf16[16,32,256]{2,1,0:T(8,128)(2,1)} %bitcast.3), calls=%async_computation | async-start | bytes 524288 | tf_op jit(solution)/shard_map/all_to_all | solution.py:58
  26.5 0.0 copy-done.1
  26.5 0.0 copy-done.2
  26.6 0.2 copy.42
  26.7 0.1 reshape.133
  26.8 0.1 copy.43
  26.9 4.2 %all-to-all-done = bf16[16,32,256]{2,1,0:T(8,128)(2,1)S(1)} async-done(((bf16[16,32,256]{2,1,0:T(8,128)(2,1)}), bf16[16,32,256]{2,1,0:T(8,128)(2,1)S(1)}, u32[]{:S(2)}, u32[]{:S(2)}) %all-to-all-start) | async-done | bytes 262176 | tf_op jit(solution)/shard_map/all_to_all | solution.py:58
  31.1 0.1 copy.40
  31.2 0.1 reshape.131
  31.3 0.1 copy.41
  31.4 0.6 gather_fusion.1
  32.1 0.6 gather_fusion
  32.7 0.2 pad_maximum_fusion
  32.9 1.5 copy.44
  34.4 7.1 %all-to-all-start.2 = ((bf16[32,16,2,1024]{3,0,2,1:T(8,128)(2,1)}), bf16[32,16,2,1024]{3,0,2,1:T(8,128)(2,1)S(1)}, u32[]{:S(2)}, u32[]{:S(2)}) async-start(bf16[32,16,2,1024]{3,0,2,1:T(8,128)(2,1)} %copy.44), calls=%async_computation.2 | async-start | bytes 4194304 | tf_op jit(solution)/shard_map/all_to_all | solution.py:18
  41.5 25.2 %all-to-all-done.2 = bf16[32,16,2,1024]{3,0,2,1:T(8,128)(2,1)S(1)} async-done(((bf16[32,16,2,1024]{3,0,2,1:T(8,128)(2,1)}), bf16[32,16,2,1024]{3,0,2,1:T(8,128)(2,1)S(1)}, u32[]{:S(2)}, u32[]{:S(2)}) %all-to-all-start.2) | async-done | bytes 2097184 | tf_op jit(solution)/shard_map/all_to_all | solution.py:18
  66.7 0.2 copy.45
  66.9 3.2 convolution_bitcast_fusion
  70.1 185.0 %all-reduce.1 = bf16[1024,1,1024]{0,2,1:T(8,128)(2,1)S(1)} all-reduce(f32[1024,1,1024]{0,2,1:T(8,128)} %convolution_bitcast_fusion), channel_id=1, replica_groups=mesh['tok'=8,'tile'=16,'pair'=2] {'tok','pair'}, use_global_device_ids=true, to_apply=%region_0.0 | all-reduce | flops 1048576 | bytes 6291456 | tf_op jit(solution)/shard_map/psum | solution.py:75
  255.1 2.6 copy.46
  257.7 0.0 all-gather.3.cloned.1.call-done
  257.7 8.2 %abs_reduce_fusion = (f32[1024]{0:T(1024)S(1)}, f32[1,1024,1024]{1,2,0:T(8,128)}) fusion(bf16[1024,1,1024]{0,2,1:T(8,128)(2,1)S(1)} %all-reduce.1, bf16[1024,1,1024]{2,0,1:T(8,128)(2,1)} %copy.46, pred[]{:T(512)S(6)} %eq.23, f32[1,1,1024,1024]{2,3,1,0:T(8,128)} %all-gather.3.cloned.1.call-done), kind=kOutput, calls=%fused_computation.12 | convolution fusion | flops 2153774080 | bytes 12587009 | tf_op jit(solution)/shard_map/kac,kbc->kab/dot_general | solution.py:83
  265.9 0.6 reduce_max.9
  267.8 2.8 divide_convert_fusion
  270.6 0.0 copy-start
  270.6 1.3 copy-done
  271.9 3.8 %fusion.36 = bf16[1024,1024]{1,0:T(8,128)(2,1)} fusion(bf16[1,1024,1024]{1,2,0:T(8,128)(2,1)S(1)} %divide_convert_fusion), kind=kOutput, calls=%fused_computation.40 | convolution fusion | flops 2153775104 | bytes 4194304 | tf_op jit(solution)/shard_map/kab,kbc->kac/dot_general | solution.py:40
  275.7 8.7 %convert_bitcast_fusion.1 = bf16[1,1024,1024]{1,2,0:T(8,128)(2,1)} fusion(bf16[1,1024,1024]{1,2,0:T(8,128)(2,1)} %copy-done, bf16[1024,1024]{1,0:T(8,128)(2,1)} %fusion.36), kind=kOutput, calls=%fused_computation.30 | convolution fusion | flops 4297064448 | bytes 6291456 | tf_op jit(solution)/shard_map/kab,kbc->kac/dot_general | solution.py:40
  284.4 6.0 %convert_bitcast_fusion = bf16[1,1024,1024]{2,1,0:T(8,128)(2,1)} fusion(bf16[1,1024,1024]{1,2,0:T(8,128)(2,1)} %convert_bitcast_fusion.1, bf16[1,1024,1024]{1,2,0:T(8,128)(2,1)} %copy-done), kind=kOutput, calls=%fused_computation.29 | convolution fusion | flops 2161115136 | bytes 6291456 | tf_op jit(solution)/shard_map/kab,kbc->kac/dot_general | solution.py:40
  290.4 0.4 collective-permute-start
  290.8 1.6 fusion.4
  292.5 43.5 %collective-permute-done = bf16[1,1024,1024]{2,1,0:T(8,128)(2,1)} collective-permute-done((bf16[1,1024,1024]{2,1,0:T(8,128)(2,1)}, bf16[1,1024,1024]{2,1,0:T(8,128)(2,1)}, u32[]{:S(2)}, u32[]{:S(2)}) %collective-permute-start) | collective-permute-done | bytes 2097184 | tf_op jit(solution)/shard_map/ppermute | solution.py:26
  335.9 3.5 multiply_reduce_fusion
  339.4 1.2 broadcast_in_dim.19
  340.7 8.5 %all-to-all-start.3 = ((f32[16,1,1]{2,1,0:T(1,128)}), f32[16,1,1]{2,1,0:T(1,128)S(1)}, u32[]{:S(2)}, u32[]{:S(2)}) async-start(f32[16,1,1]{2,1,0:T(1,128)} %broadcast_in_dim.19), calls=%async_computation.3 | async-start | bytes 16384 | tf_op jit(solution)/shard_map/all_to_all | solution.py:31
  349.2 1.1 constant_dynamic-slice_fusion
  350.3 1.0 copy.49
  351.3 7.9 %all-to-all-done.3 = f32[16,1,1]{2,1,0:T(1,128)S(1)} async-done(((f32[16,1,1]{2,1,0:T(1,128)}), f32[16,1,1]{2,1,0:T(1,128)S(1)}, u32[]{:S(2)}, u32[]{:S(2)}) %all-to-all-start.3) | async-done | bytes 96 | tf_op jit(solution)/shard_map/all_to_all | solution.py:31
  359.2 0.6 reduce_sum.29
  361.1 0.7 fusion.44
  (2 shorter events, 0.0 us)
Async XLA Ops:
  7.2 19.4 %copy-start.1 = (s32[16]{0:T(128)S(1)}, s32[16]{0:T(128)}, u32[]{:S(2)}) copy-start(s32[16]{0:T(128)} %constant.59) | copy-start | bytes 196
  7.2 19.4 %copy-start.2 = (s32[16]{0:T(128)S(1)}, s32[16]{0:T(128)}, u32[]{:S(2)}) copy-start(s32[16]{0:T(128)} %constant.58) | copy-start | bytes 196
  7.2 250.5 %all-gather.3.cloned.1.call-start = ((), (), s32[]{:S(2)}) async-start(), calls=%async_computation.4 | async-start | bytes 4718592 | tf_op jit(solution)/shard_map/all_gather | solution.py:82
  19.6 11.5 %all-to-all-start = ((bf16[16,32,256]{2,1,0:T(8,128)(2,1)}), bf16[16,32,256]{2,1,0:T(8,128)(2,1)S(1)}, u32[]{:S(2)}, u32[]{:S(2)}) async-start(bf16[16,32,256]{2,1,0:T(8,128)(2,1)} %bitcast.3), calls=%async_computation | async-start | bytes 524288 | tf_op jit(solution)/shard_map/all_to_all | solution.py:58
  34.4 32.3 %all-to-all-start.2 = ((bf16[32,16,2,1024]{3,0,2,1:T(8,128)(2,1)}), bf16[32,16,2,1024]{3,0,2,1:T(8,128)(2,1)S(1)}, u32[]{:S(2)}, u32[]{:S(2)}) async-start(bf16[32,16,2,1024]{3,0,2,1:T(8,128)(2,1)} %copy.44), calls=%async_computation.2 | async-start | bytes 4194304 | tf_op jit(solution)/shard_map/all_to_all | solution.py:18
  270.6 1.3 copy-start
  290.4 45.5 %collective-permute-start = (bf16[1,1024,1024]{2,1,0:T(8,128)(2,1)}, bf16[1,1024,1024]{2,1,0:T(8,128)(2,1)}, u32[]{:S(2)}, u32[]{:S(2)}) collective-permute-start(bf16[1,1024,1024]{2,1,0:T(8,128)(2,1)} %convert_bitcast_fusion), channel_id=1, source_target_pairs={{0,1},{1,0},{2,3},{3,2},{4,5},{5,4},{6,7},{7,6},{8,9},{9,8},{10,11... | collective-permute-start | bytes 6291464 | tf_op jit(solution)/shard_map/ppermute | solution.py:26
  340.7 18.5 %all-to-all-start.3 = ((f32[16,1,1]{2,1,0:T(1,128)}), f32[16,1,1]{2,1,0:T(1,128)S(1)}, u32[]{:S(2)}, u32[]{:S(2)}) async-start(f32[16,1,1]{2,1,0:T(1,128)} %broadcast_in_dim.19), calls=%async_computation.3 | async-start | bytes 16384 | tf_op jit(solution)/shard_map/all_to_all | solution.py:31
Sparse Core Ops, SparseCore 0:
  10.3 65.1 all-gather.2
where the time goes:
time: 369 us
  blocking collectives  195 us (53%)
  waiting for transfers between devices  80.7 us (22%)
  matrix products  33.4 us (9%)
  starting transfers between devices  23.1 us (6%)
  between operations  16.7 us (5%)
  local copies, waits for them, and re-layouts  12.9 us (3%)
  other arithmetic  6.52 us (2%)
    psum x1, blocking collectives, per_device(): gradient = lax.psum(partial_grad, ('tok', 'pair')).astype(jnp.bfloat16)  185 us
    ppermute x1, waiting for transfers between devices, swapped(): lax.ppermute(shard, axis, [(i, i ^ 1 << stride) for i in range(lax.axis_s...  43.5 us
    all_to_all x1, waiting for transfers between devices, in_one_piece(): lax.all_to_all(both, axis, split_axis=split_dim, concat_axis=concat_dim,...  25.2 us
    dot_general x3, matrix products, product_bf(): jnp.einsum('kab,kbc->kac', left_part, right_part, preferred_element_type=...  18.5 us
    all_to_all x1, blocking collectives, per_device(): lax.all_to_all(output_grads, 'tile', split_axis=0, concat_axis=1, tiled=T...  10.3 us
    all_to_all x1, starting transfers between devices, copy_for_each(): return lax.all_to_all(copies, axis, split_axis=0, concat_axis=0, tiled=True)  8.54 us
    dot_general x1, matrix products, per_device(): jnp.einsum('kac,kbc->kab', factor_data, factor_data, preferred_element_ty...  8.16 us
    all_to_all x1, waiting for transfers between devices, copy_for_each(): return lax.all_to_all(copies, axis, split_axis=0, concat_axis=0, tiled=True)  7.88 us
  transfers between devices with their start and end apart: 5, of which 4 were waited for; matrix products, arithmetic and copies ran while one was open for 4% of the time, Pallas kernels for 0%

commit v1 on v0

--- a/solution.py
+++ b/solution.py
@@ -72,7 +72,7 @@
     partial_grad = jnp.einsum(
         "ktr,ktc->rkc", left_acts, right_cots, preferred_element_type=jnp.float32
     )
-    gradient = lax.psum(partial_grad, ("tok", "pair")).astype(jnp.bfloat16)
+    gradient = lax.psum(lax.psum(partial_grad, "pair"), "tok").astype(jnp.bfloat16)
     grad_sq = jnp.einsum("rkc,rkc->k", gradient, gradient, preferred_element_type=jnp.float32)
     by_rows = jnp.transpose(gradient, (1, 0, 2))
     by_cols = jnp.transpose(gradient, (1, 2, 0))

time: 369 us -> 392 us (1.062)
  waiting for transfers between devices: 80.7 us -> 177 us
  blocking collectives: 195 us -> 130 us
  starting transfers between devices: 23.1 us -> 13.9 us
    psum x0 -> x1, waiting for transfers between devices: none -> 122 us  [per_device(): lax.psum(partial_grad, 'pair')]
    psum x1, blocking collectives: 185 us -> 89.1 us  [per_device(): lax.psum(lax.psum(partial_grad, 'pair'), 'tok').astype(jnp.bfloat16)]
    all_to_all x0 -> x1, blocking collectives: none -> 30.3 us  [in_one_piece(): lax.all_to_all(both, axis, split_axis=split_dim, concat_axis=concat_dim,...]
    all_to_all x1 -> x0, waiting for transfers between devices: 25.2 us -> none  [in_one_piece(): lax.all_to_all(both, axis, split_axis=split_dim, concat_axis=concat_dim,...]
    all_to_all x1 -> x0, starting transfers between devices: 7.15 us -> none  [in_one_piece(): lax.all_to_all(both, axis, split_axis=split_dim, concat_axis=concat_dim,...]
  transfers between devices with their start and end apart: 5 -> 5, of which waited for: 4 -> 4; matrix products, arithmetic and copies ran while one was open for 4% -> 2% of each run, Pallas kernels for 0% -> 0%
where the time goes in v1:
time: 392 us
  waiting for transfers between devices  177 us (45%)
  blocking collectives  130 us (33%)
  matrix products  33.4 us (9%)
  between operations  18.2 us (5%)
  starting transfers between devices  13.9 us (4%)
  local copies, waits for them, and re-layouts  11.7 us (3%)
  other arithmetic  7.83 us (2%)
    psum x1, waiting for transfers between devices, per_device(): lax.psum(partial_grad, 'pair')  122 us
    psum x1, blocking collectives, per_device(): lax.psum(lax.psum(partial_grad, 'pair'), 'tok').astype(jnp.bfloat16)  89.1 us
    ppermute x1, waiting for transfers between devices, swapped(): lax.ppermute(shard, axis, [(i, i ^ 1 << stride) for i in range(lax.axis_s...  44.5 us
    all_to_all x1, blocking collectives, in_one_piece(): lax.all_to_all(both, axis, split_axis=split_dim, concat_axis=concat_dim,...  30.3 us
    dot_general x3, matrix products, product_bf(): jnp.einsum('kab,kbc->kac', left_part, right_part, preferred_element_type=...  18.5 us
    all_to_all x1, blocking collectives, per_device(): lax.all_to_all(output_grads, 'tile', split_axis=0, concat_axis=1, tiled=T...  10.3 us
    dot_general x1, matrix products, per_device(): jnp.einsum('kac,kbc->kab', factor_data, factor_data, preferred_element_ty...  8.16 us
    all_to_all x1, waiting for transfers between devices, copy_for_each(): return lax.all_to_all(copies, axis, split_axis=0, concat_axis=0, tiled=True)  7.88 us
  transfers between devices with their start and end apart: 5, of which 4 were waited for; matrix products, arithmetic and copies ran while one was open for 2% of the time, Pallas kernels for 0%

profile of v1, /device:TPU:18, one launch (start us, length us, event | category | flops | bytes accessed | tf_op | source)
XLA Modules:
  0.0 391.7 jit_solution(2801614974646752032)
XLA Ops:
  8.0 10.3 %all_to_all.56 = bf16[16,32,256]{2,1,0:T(8,128)(2,1)S(1)} all-to-all(bf16[16,32,256]{2,1,0:T(8,128)(2,1)} %bitcast.102), channel_id=1, replica_groups=mesh['tok'=8,'tile'=16,'pair'=2] {'tile'}, dimensions={0} | all-to-all | bytes 524288 | tf_op jit(solution)/shard_map/all_to_all | solution.py:59
  18.3 7.0 %all-to-all-start = ((bf16[16,32,256]{2,1,0:T(8,128)(2,1)}), bf16[16,32,256]{2,1,0:T(8,128)(2,1)S(1)}, u32[]{:S(2)}, u32[]{:S(2)}) async-start(bf16[16,32,256]{2,1,0:T(8,128)(2,1)} %bitcast.103), calls=%async_computation | async-start | bytes 524288 | tf_op jit(solution)/shard_map/all_to_all | solution.py:58
  25.2 0.0 all-reduce.3.cloned.1.call-start
  25.3 0.7 pad_clamp_fusion
  25.9 0.7 pad_clamp_fusion.1
  26.6 0.1 copy.42
  26.7 0.1 reshape.133
  26.8 0.1 copy.43
  26.9 2.8 all-to-all-done
  29.8 0.1 copy.40
  29.9 0.1 reshape.131
  30.0 0.1 copy.41
  30.1 0.6 gather_fusion.1
  30.8 0.6 gather_fusion
  31.4 0.2 pad_maximum_fusion
  31.6 0.3 copy.44
  31.9 30.3 %all_to_all.57 = bf16[32,16,2,1024]{3,0,2,1:T(8,128)(2,1)S(1)} all-to-all(bf16[32,16,2,1024]{3,0,2,1:T(8,128)(2,1)S(1)} %copy.44), channel_id=1, replica_groups=mesh['tok'=8,'tile'=16,'pair'=2] {'tile'}, dimensions={1} | all-to-all | bytes 4194304 | tf_op jit(solution)/shard_map/all_to_all | solution.py:18
  62.1 0.3 copy.45
  62.4 3.3 convolution_bitcast_fusion
  65.7 0.0 copy-start.1
  65.7 0.0 all-reduce.3.cloned.1.call-update
  65.7 0.0 all-gather.3.cloned.1.call-start
  65.8 1.0 copy-done.1
  66.7 1.0 copy.39
  67.7 0.0 all-gather.3.cloned.1.call-update
  67.8 121.8 %all-reduce.3.cloned.1.call-done = f32[1024,1,1024]{0,2,1:T(8,128)} async-done(((f32[1024,1,1024]{0,2,1:T(8,128)}), f32[1024,1,1024]{0,2,1:T(8,128)}) %all-reduce.3.cloned.1.call-update) | async-done | bytes 4194320 | tf_op jit(solution)/shard_map/psum | solution.py:75
  189.5 89.1 %all-reduce.4 = bf16[1024,1,1024]{0,2,1:T(8,128)(2,1)S(1)} all-reduce(f32[1024,1,1024]{0,2,1:T(8,128)} %all-reduce.3.cloned.1.call-done), channel_id=1, replica_groups=mesh['tok'=8,'tile'=16,'pair'=2] {'tok'}, use_global_device_ids=true, to_apply=%region_1.0 | all-reduce | flops 1048576 | bytes 6291456 | tf_op jit(solution)/shard_map/psum | solution.py:75
  278.6 2.6 copy.46
  281.3 0.0 all-gather.3.cloned.1.call-done
  281.3 8.2 %abs_reduce_fusion = (f32[1024]{0:T(1024)S(1)}, f32[1,1024,1024]{1,2,0:T(8,128)}) fusion(bf16[1024,1,1024]{0,2,1:T(8,128)(2,1)S(1)} %all-reduce.4, bf16[1024,1,1024]{2,0,1:T(8,128)(2,1)} %copy.46, pred[]{:T(512)S(6)} %eq.23, f32[1,1,1024,1024]{2,3,1,0:T(8,128)} %all-gather.3.cloned.1.call-done), kind=kOutput, calls=%fused_computation.12 | convolution fusion | flops 2153774080 | bytes 12587009 | tf_op jit(solution)/shard_map/kac,kbc->kab/dot_general | solution.py:83
  289.4 0.6 reduce_max.9
  291.3 2.8 divide_convert_fusion
  294.1 0.0 copy-start
  294.1 1.3 copy-done
  295.4 3.8 fusion.36
  299.2 8.7 %convert_bitcast_fusion.1 = bf16[1,1024,1024]{1,2,0:T(8,128)(2,1)} fusion(bf16[1,1024,1024]{1,2,0:T(8,128)(2,1)} %copy-done, bf16[1024,1024]{1,0:T(8,128)(2,1)} %fusion.36), kind=kOutput, calls=%fused_computation.30 | convolution fusion | flops 4297064448 | bytes 6291456 | tf_op jit(solution)/shard_map/kab,kbc->kac/dot_general | solution.py:40
  307.9 6.0 %convert_bitcast_fusion = bf16[1,1024,1024]{2,1,0:T(8,128)(2,1)} fusion(bf16[1,1024,1024]{1,2,0:T(8,128)(2,1)} %convert_bitcast_fusion.1, bf16[1,1024,1024]{1,2,0:T(8,128)(2,1)} %copy-done), kind=kOutput, calls=%fused_computation.29 | convolution fusion | flops 2161115136 | bytes 6291456 | tf_op jit(solution)/shard_map/kab,kbc->kac/dot_general | solution.py:40
  313.9 1.5 collective-permute-start
  315.4 1.6 fusion.4
  317.0 44.5 %collective-permute-done = bf16[1,1024,1024]{2,1,0:T(8,128)(2,1)} collective-permute-done((bf16[1,1024,1024]{2,1,0:T(8,128)(2,1)}, bf16[1,1024,1024]{2,1,0:T(8,128)(2,1)}, u32[]{:S(2)}, u32[]{:S(2)}) %collective-permute-start) | collective-permute-done | bytes 2097184 | tf_op jit(solution)/shard_map/ppermute | solution.py:26
  361.5 3.5 multiply_reduce_fusion
  365.0 1.2 broadcast_in_dim.19
  366.3 5.4 %all-to-all-start.3 = ((f32[16,1,1]{2,1,0:T(1,128)}), f32[16,1,1]{2,1,0:T(1,128)S(1)}, u32[]{:S(2)}, u32[]{:S(2)}) async-start(f32[16,1,1]{2,1,0:T(1,128)} %broadcast_in_dim.19), calls=%async_computation.3 | async-start | bytes 16384 | tf_op jit(solution)/shard_map/all_to_all | solution.py:31
  371.7 1.1 constant_dynamic-slice_fusion
  372.8 1.0 copy.49
  373.8 7.9 %all-to-all-done.3 = f32[16,1,1]{2,1,0:T(1,128)S(1)} async-done(((f32[16,1,1]{2,1,0:T(1,128)}), f32[16,1,1]{2,1,0:T(1,128)S(1)}, u32[]{:S(2)}, u32[]{:S(2)}) %all-to-all-start.3) | async-done | bytes 96 | tf_op jit(solution)/shard_map/all_to_all | solution.py:31
  381.7 0.6 reduce_sum.29
  383.5 0.7 fusion.44
Async XLA Ops:
  18.3 11.5 %all-to-all-start = ((bf16[16,32,256]{2,1,0:T(8,128)(2,1)}), bf16[16,32,256]{2,1,0:T(8,128)(2,1)S(1)}, u32[]{:S(2)}, u32[]{:S(2)}) async-start(bf16[16,32,256]{2,1,0:T(8,128)(2,1)} %bitcast.103), calls=%async_computation | async-start | bytes 524288 | tf_op jit(solution)/shard_map/all_to_all | solution.py:58
  25.2 164.3 %all-reduce.3.cloned.1.call-start = ((), (), s32[]{:S(2)}) async-start(), calls=%async_computation.4 | async-start | bytes 8388608 | tf_op jit(solution)/shard_map/psum | solution.py:75
  65.7 1.0 copy-start.1
  65.7 215.6 %all-gather.3.cloned.1.call-start = ((), (), s32[]{:S(2)}) async-start(), calls=%async_computation.5 | async-start | bytes 4718592 | tf_op jit(solution)/shard_map/all_gather | solution.py:82
  294.1 1.3 copy-start
  313.9 47.6 %collective-permute-start = (bf16[1,1024,1024]{2,1,0:T(8,128)(2,1)}, bf16[1,1024,1024]{2,1,0:T(8,128)(2,1)}, u32[]{:S(2)}, u32[]{:S(2)}) collective-permute-start(bf16[1,1024,1024]{2,1,0:T(8,128)(2,1)} %convert_bitcast_fusion), channel_id=1, source_target_pairs={{0,1},{1,0},{2,3},{3,2},{4,5},{5,4},{6,7},{7,6},{8,9},{9,8},{10,11... | collective-permute-start | bytes 6291464 | tf_op jit(solution)/shard_map/ppermute | solution.py:26
  366.3 15.4 %all-to-all-start.3 = ((f32[16,1,1]{2,1,0:T(1,128)}), f32[16,1,1]{2,1,0:T(1,128)S(1)}, u32[]{:S(2)}, u32[]{:S(2)}) async-start(f32[16,1,1]{2,1,0:T(1,128)} %broadcast_in_dim.19), calls=%async_computation.3 | async-start | bytes 16384 | tf_op jit(solution)/shard_map/all_to_all | solution.py:31
Sparse Core Ops, SparseCore 0:
  65.8 123.6 all-reduce.2
Sparse Core Ops, SparseCore 1:
  68.5 65.5 all-gather.2
